TPU v7x, 32 devices: a whole 2x2x4 slice. The times are simulated.
32 devices in a mesh: dp: 8 (over z, y), tensor: 4 (over x, core).
Axes of the slice: x: 2, y: 2, z: 4, core: 2. Of those that a mesh axis runs over, the one named last changes fastest.
Arguments:
- tokens: bfloat16 [16384, 768], P('dp'), may hold values from -6 to 6
- cotangent: bfloat16 [16384, 768], P('dp'), may hold values from -6 to 6
- counts: int32 [16, 5], P('dp'), may hold values from 0 to 576, as said below
- sides: int32 [16, 5], P('dp'), may hold values from 0 to 24, as said below
- segments: int32 [16384], P('dp'), may hold values from 0 to 5, as said below
- norm1_gain: float32 [768], replicated, may hold values from 0.5 to 1.5
- norm1_shift: float32 [768], replicated, may hold values from -3 to 3
- w_qkv: bfloat16 [768, 3, 768], P(None, None, 'tensor'), may hold values from -0.21875 to 0.21875
- b_qkv: float32 [3, 768], P(None, 'tensor'), may hold values from -3 to 3
- freqs: float32 [12, 2, 32], P('tensor'), may hold values from -2 to 2
- w_out: bfloat16 [768, 768], P('tensor'), may hold values from -1.5 to 1.5
- b_out: float32 [768], replicated, may hold values from -3 to 3
- norm2_gain: float32 [768], replicated, may hold values from 0.5 to 1.5
- norm2_shift: float32 [768], replicated, may hold values from -3 to 3
- w_fc1: bfloat16 [768, 3072], P(None, 'tensor'), may hold values from -0.21875 to 0.21875
- b_fc1: float32 [3072], P('tensor'), may hold values from -3 to 3
- w_fc2: bfloat16 [3072, 768], P('tensor'), may hold values from -0.109375 to 0.109375
- b_fc2: float32 [768], replicated, may hold values from -3 to 3
Outputs:
- block_output: bfloat16 [16384, 768], P('dp')
- token_grad: float32 [16384, 768], P('dp')
- norm1_gain_grad: float32 [768], replicated
- norm1_shift_grad: float32 [768], replicated
- qkv_grad: float32 [768, 3, 768], P(None, None, 'tensor')
- qkv_bias_grad: float32 [3, 768], P(None, 'tensor')
- freqs_grad: float32 [12, 2, 32], P('tensor')
- out_grad: float32 [768, 768], P('tensor')
- out_bias_grad: float32 [768], replicated
- norm2_gain_grad: float32 [768], replicated
- norm2_shift_grad: float32 [768], replicated
- fc1_grad: float32 [768, 3072], P(None, 'tensor')
- fc1_bias_grad: float32 [3072], P('tensor')
- fc2_grad: float32 [3072, 768], P('tensor')
- fc2_bias_grad: float32 [768], replicated
Inputs may be any that keep to these rules, and one draw needn't show every extreme that they name: `counts`: A used image slot holds the square of its side; unused slots hold 0 and come after the used ones; a pack's total is under 1024. `sides`: side of each image's square patch grid; 0 for an unused slot. `segments`: each image lies whole in its pack from the pack's first slot on, in slot order and row-major patch order; slots after the last image hold 5 (padding).
All inputs are finite; a program needn't handle non-finite values.
Results may differ from a plain program's by a relative error of at most 0.014.
Values may be sent and summed in bfloat16 or wider, within the bound.
A program may use at most 128 MiB of HBM per device.

v0:
```python
import jax
import jax.numpy as jnp
from jax import lax
from jax.sharding import PartitionSpec as P


def layer_stats(values_in, norm_gain, norm_shift):
    center = values_in - jnp.mean(values_in, axis=-1, keepdims=True)
    inverse = lax.rsqrt(jnp.mean(center * center, axis=-1, keepdims=True) + 1e-06)
    scaled = center * inverse
    return (scaled * norm_gain + norm_shift, scaled, inverse)


def norm_back(grad_normed, scaled, inverse, norm_gain):
    grad_scaled = grad_normed * norm_gain
    return inverse * (
        grad_scaled
        - jnp.mean(grad_scaled, axis=-1, keepdims=True)
        - scaled * jnp.mean(grad_scaled * scaled, axis=-1, keepdims=True)
    )


def positions(segment_ids, image_counts, image_sides):
    slot_count = image_counts.shape[0]
    starts = jnp.cumsum(image_counts, dtype=jnp.int32) - image_counts
    matched = segment_ids[:, None] == jnp.arange(slot_count, dtype=jnp.int32)[None, :]
    start_tok = jnp.sum(jnp.where(matched, starts[None, :], 0), axis=1)
    side_tok = jnp.sum(jnp.where(matched, image_sides[None, :], 0), axis=1)
    live_slot = segment_ids < slot_count
    slot_index = jnp.arange(segment_ids.shape[0], dtype=jnp.int32)
    patch_index = jnp.where(live_slot, slot_index - start_tok, 0)
    side_tok = jnp.where(live_slot, side_tok, 1)
    row_index = patch_index // side_tok
    col_index = patch_index - row_index * side_tok
    return (col_index.astype(jnp.float32), row_index.astype(jnp.float32))


def rotate_pairs(rotate_in, freq_table, col_pos, row_pos):
    half_size = rotate_in.shape[-1] // 2
    angles = (
        col_pos[:, None, None] * freq_table[None, :, 0, :]
        + row_pos[:, None, None] * freq_table[None, :, 1, :]
    )
    cosine = jnp.cos(angles)[:, None]
    sine_part = jnp.sin(angles)[:, None]
    first_half = rotate_in[..., :half_size]
    second_half = rotate_in[..., half_size:]
    return jnp.concatenate(
        [
            first_half * cosine - second_half * sine_part,
            first_half * sine_part + second_half * cosine,
        ],
        axis=-1,
    )


def attend_forward(queries, keys, values_v, segment_ids, block_rows):
    row_total, head_count, head_size = queries.shape
    score_scale = head_size ** (-0.5)

    def one_block(pieces):
        query_blk, segment_blk = pieces
        scores = (
            jnp.einsum("qhd,khd->hqk", query_blk, keys, preferred_element_type=jnp.float32)
            * score_scale
        )
        allowed = segment_blk[:, None] == segment_ids[None, :]
        scores = jnp.where(allowed[None], scores, -1e30)
        row_top = jnp.max(scores, axis=-1, keepdims=True)
        exponent = jnp.exp(scores - row_top)
        row_sum = jnp.sum(exponent, axis=-1, keepdims=True)
        soft_weights = (exponent / row_sum).astype(jnp.bfloat16)
        mixed = jnp.einsum(
            "hqk,khd->qhd", soft_weights, values_v, preferred_element_type=jnp.float32
        )
        return (mixed.astype(jnp.bfloat16), (row_top + jnp.log(row_sum))[..., 0])

    blocks = (
        queries.reshape(row_total // block_rows, block_rows, head_count, head_size),
        segment_ids.reshape(row_total // block_rows, block_rows),
    )
    mixed_heads, log_totals = lax.map(one_block, blocks)
    return (mixed_heads.reshape(row_total, head_count * head_size), log_totals)


def attend_backward(queries, keys, values_v, grad_heads, log_totals, segment_ids, block_rows):
    row_total, head_count, head_size = queries.shape
    score_scale = head_size ** (-0.5)

    def one_block(carried, pieces):
        grad_keys, grad_values = carried
        query_blk, grad_blk, total_blk, segment_blk = pieces
        scores = (
            jnp.einsum("qhd,khd->hqk", query_blk, keys, preferred_element_type=jnp.float32)
            * score_scale
        )
        allowed = segment_blk[:, None] == segment_ids[None, :]
        soft_weights = jnp.where(allowed[None], jnp.exp(scores - total_blk[..., None]), 0.0)
        low_weights = soft_weights.astype(jnp.bfloat16)
        grad_weights = jnp.einsum(
            "qhd,khd->hqk", grad_blk, values_v, preferred_element_type=jnp.float32
        )
        inner_sum = jnp.sum(grad_weights * soft_weights, axis=-1, keepdims=True)
        grad_scores = (soft_weights * (grad_weights - inner_sum)).astype(jnp.bfloat16)
        grad_query = (
            jnp.einsum("hqk,khd->qhd", grad_scores, keys, preferred_element_type=jnp.float32)
            * score_scale
        )
        grad_keys = (
            grad_keys
            + jnp.einsum("hqk,qhd->khd", grad_scores, query_blk, preferred_element_type=jnp.float32)
            * score_scale
        )
        grad_values = grad_values + jnp.einsum(
            "hqk,qhd->khd", low_weights, grad_blk, preferred_element_type=jnp.float32
        )
        return ((grad_keys, grad_values), grad_query)

    block_count = row_total // block_rows
    zero_init = jnp.zeros((row_total, head_count, head_size), jnp.float32)
    pieces = (
        queries.reshape(block_count, block_rows, head_count, head_size),
        grad_heads.reshape(block_count, block_rows, head_count, head_size),
        log_totals,
        segment_ids.reshape(block_count, block_rows),
    )
    (grad_keys, grad_values), grad_queries = lax.scan(one_block, (zero_init, zero_init), pieces)
    return (grad_queries.reshape(row_total, head_count, head_size), grad_keys, grad_values)


def on_device(
    tokens,
    cotangent,
    counts,
    sides,
    segments,
    norm1_gain,
    norm1_shift,
    w_qkv,
    b_qkv,
    freqs,
    w_out,
    b_out,
    norm2_gain,
    norm2_shift,
    w_fc1,
    b_fc1,
    w_fc2,
    b_fc2,
):
    row_total = tokens.shape[0]
    pack_count = counts.shape[0]
    pack_rows = row_total // pack_count
    head_count = freqs.shape[0]
    local_width = w_qkv.shape[2]
    head_size = local_width // head_count
    block_rows = min(512, pack_rows)
    segment_packs = segments.reshape(pack_count, pack_rows)
    col_packs, row_packs = jax.vmap(positions)(segment_packs, counts, sides)
    col_pos = col_packs.reshape(row_total)
    row_pos = row_packs.reshape(row_total)
    residual = tokens.astype(jnp.float32)
    normed_one, scaled_one, inverse_one = layer_stats(residual, norm1_gain, norm1_shift)
    low_normed_one = normed_one.astype(jnp.bfloat16)
    projected = (
        jnp.einsum("td,dcj->tcj", low_normed_one, w_qkv, preferred_element_type=jnp.float32)
        + b_qkv[None]
    )
    rotate_in = projected[:, :2].reshape(row_total, 2, head_count, head_size)

    def turn(pairs_in, freq_table):
        return rotate_pairs(pairs_in, freq_table, col_pos, row_pos)

    turned = turn(rotate_in, freqs)
    queries = turned[:, 0].astype(jnp.bfloat16)
    keys = turned[:, 1].astype(jnp.bfloat16)
    values_v = projected[:, 2].reshape(row_total, head_count, head_size).astype(jnp.bfloat16)
    pack_shape = (pack_count, pack_rows, head_count, head_size)
    query_packs = queries.reshape(pack_shape)
    key_packs = keys.reshape(pack_shape)
    value_packs = values_v.reshape(pack_shape)

    def forward_pack(pieces):
        return attend_forward(pieces[0], pieces[1], pieces[2], pieces[3], block_rows)

    mixed_packs, log_totals = lax.map(
        forward_pack, (query_packs, key_packs, value_packs, segment_packs)
    )
    mixed_heads = mixed_packs.reshape(row_total, local_width)
    partial_attn = jnp.dot(mixed_heads, w_out, preferred_element_type=jnp.float32)
    middle = residual + lax.psum(partial_attn, "tensor") + b_out
    normed_two, scaled_two, inverse_two = layer_stats(middle, norm2_gain, norm2_shift)
    low_normed_two = normed_two.astype(jnp.bfloat16)
    hidden_pre = jnp.dot(low_normed_two, w_fc1, preferred_element_type=jnp.float32) + b_fc1
    hidden = jax.nn.gelu(hidden_pre, approximate=False).astype(jnp.bfloat16)
    partial_mlp = jnp.dot(hidden, w_fc2, preferred_element_type=jnp.float32)
    block_output = (
        middle + lax.psum(partial_mlp.astype(jnp.bfloat16), "tensor").astype(jnp.float32) + b_fc2
    ).astype(jnp.bfloat16)
    grad_output = cotangent.astype(jnp.float32)
    grad_fc2_bias = jnp.sum(grad_output, axis=0)
    grad_fc2 = jnp.einsum("tf,td->fd", hidden, cotangent, preferred_element_type=jnp.float32)
    grad_hidden = jnp.einsum("td,fd->tf", cotangent, w_fc2, preferred_element_type=jnp.float32)
    unused, gelu_pull = jax.vjp(
        lambda pre_values: jax.nn.gelu(pre_values, approximate=False), hidden_pre
    )
    grad_pre = gelu_pull(grad_hidden)[0].astype(jnp.bfloat16)
    grad_fc1_bias = jnp.sum(grad_pre.astype(jnp.float32), axis=0)
    grad_fc1 = jnp.einsum("td,tf->df", low_normed_two, grad_pre, preferred_element_type=jnp.float32)
    partial_norm_two = jnp.einsum("tf,df->td", grad_pre, w_fc1, preferred_element_type=jnp.float32)
    grad_normed_two = lax.psum(partial_norm_two, "tensor")
    grad_middle = grad_output + norm_back(grad_normed_two, scaled_two, inverse_two, norm2_gain)
    low_grad_middle = grad_middle.astype(jnp.bfloat16)
    grad_gain_two = jnp.sum(grad_normed_two * scaled_two, axis=0)
    grad_shift_two = jnp.sum(grad_normed_two, axis=0)
    grad_out_bias = jnp.sum(low_grad_middle.astype(jnp.float32), axis=0)
    grad_out_weight = jnp.einsum(
        "tj,td->jd", mixed_heads, low_grad_middle, preferred_element_type=jnp.float32
    )
    grad_mixed = jnp.einsum("td,jd->tj", low_grad_middle, w_out, preferred_element_type=jnp.float32)
    grad_mixed = grad_mixed.astype(jnp.bfloat16).reshape(pack_shape)

    def backward_pack(pieces):
        return attend_backward(
            pieces[0], pieces[1], pieces[2], pieces[3], pieces[4], pieces[5], block_rows
        )

    grad_query_packs, grad_key_packs, grad_value_packs = lax.map(
        backward_pack, (query_packs, key_packs, value_packs, grad_mixed, log_totals, segment_packs)
    )
    grad_queries = grad_query_packs.reshape(row_total, head_count, head_size)
    grad_keys = grad_key_packs.reshape(row_total, head_count, head_size)
    grad_values = grad_value_packs.reshape(row_total, head_count, head_size)
    unused, rotate_pull = jax.vjp(turn, rotate_in, freqs)
    grad_rotate_in, grad_freqs = rotate_pull(jnp.stack([grad_queries, grad_keys], axis=1))
    grad_projected = jnp.concatenate(
        [
            grad_rotate_in.reshape(row_total, 2, local_width),
            grad_values.reshape(row_total, 1, local_width),
        ],
        axis=1,
    ).astype(jnp.bfloat16)
    grad_qkv_bias = jnp.sum(grad_projected.astype(jnp.float32), axis=0)
    grad_qkv = jnp.einsum(
        "td,tcj->dcj", low_normed_one, grad_projected, preferred_element_type=jnp.float32
    )
    partial_norm_one = jnp.einsum(
        "tcj,dcj->td", grad_projected, w_qkv, preferred_element_type=jnp.float32
    )
    grad_normed_one = lax.psum(partial_norm_one.astype(jnp.bfloat16), "tensor").astype(jnp.float32)
    token_grad = grad_middle + norm_back(grad_normed_one, scaled_one, inverse_one, norm1_gain)
    grad_gain_one = jnp.sum(grad_normed_one * scaled_one, axis=0)
    grad_shift_one = jnp.sum(grad_normed_one, axis=0)
    summed = lax.psum(
        (
            grad_gain_one,
            grad_shift_one,
            grad_qkv,
            grad_qkv_bias,
            grad_freqs,
            grad_out_weight,
            grad_out_bias,
            grad_gain_two,
            grad_shift_two,
            grad_fc1,
            grad_fc1_bias,
            grad_fc2,
            grad_fc2_bias,
        ),
        "dp",
    )
    return (
        block_output,
        token_grad,
        summed[0],
        summed[1],
        summed[2],
        summed[3],
        summed[4],
        summed[5],
        summed[6],
        summed[7],
        summed[8],
        summed[9],
        summed[10],
        summed[11],
        summed[12],
    )


def solution(mesh):
    in_specs = (
        P("dp", None),
        P("dp", None),
        P("dp", None),
        P("dp", None),
        P("dp"),
        P(),
        P(),
        P(None, None, "tensor"),
        P(None, "tensor"),
        P("tensor", None, None),
        P("tensor", None),
        P(),
        P(),
        P(),
        P(None, "tensor"),
        P("tensor"),
        P("tensor", None),
        P(),
    )
    out_specs = (
        P("dp", None),
        P("dp", None),
        P(),
        P(),
        P(None, None, "tensor"),
        P(None, "tensor"),
        P("tensor", None, None),
        P("tensor", None),
        P(),
        P(),
        P(),
        P(None, "tensor"),
        P("tensor"),
        P("tensor", None),
        P(),
    )
    return jax.shard_map(
        on_device, mesh=mesh, in_specs=in_specs, out_specs=out_specs, check_vma=False
    )
```

profile of v0, /device:TPU:0, one launch (start us, length us, event | category | flops | bytes accessed | tf_op | source)
XLA Modules:
  0.0 858.8 jit_solution(9181087721669908261)
XLA Ops:
  29.6 33.4 %while.54 = (s32[]{:T(128)}, bf16[2,1024,192]{1,2,0:T(8,128)(2,1)}, f32[2,2,3,512]{3,2,1,0:T(4,128)}, bf16[2,1024,3,64]{1,3,2,0:T(8,128)(2,1)}, s32[2,1024]{1,0:...) while((s32[]{:T(128)}, bf16[2,1024,192]{1,2,0:T(8,128)(2,1)}, ...), condition=%wide.region_10.11_spmd, body=%wide.region_5.10_spmd.sunk | while | flops 422148608 | bytes 28762504 | solution.py:186
  33.6 11.3 %while.57 = (s32[]{:T(128)}, bf16[2,512,3,64]{1,3,2,0:T(8,128)(2,1)S(1)}, f32[2,3,512]{2,1,0:T(4,128)S(1)}, s32[2,512]{1,0:T(2,128)S(1)}, s32[1024]{0:T(1024)S(1...) while((s32[]{:T(128)}, ...), condition=%wide.region_9.9_spmd, body=%wide.region_6.8_spmd.sunk | while | flops 422148608 | bytes 22220916 | solution.py:82
  50.2 11.3 %while.57 = (s32[]{:T(128)}, bf16[2,512,3,64]{1,3,2,0:T(8,128)(2,1)S(1)}, f32[2,3,512]{2,1,0:T(4,128)S(1)}, s32[2,512]{1,0:T(2,128)S(1)}, s32[1024]{0:T(1024)S(1...) while((s32[]{:T(128)}, ...), condition=%wide.region_9.9_spmd, body=%wide.region_6.8_spmd.sunk | while | flops 422148608 | bytes 22220916 | solution.py:82
  65.2 3.7 fusion.84
  69.0 122.4 %all-reduce.12.cloned.1.call-done = f32[2048,768]{1,0:T(8,128)} async-done(((f32[2048,768]{1,0:T(8,128)}), f32[2048,768]{1,0:T(8,128)}) %all-reduce.12.cloned.1.call-update) | async-done | bytes 6291472 | tf_op jit(solution)/shard_map/psum | solution.py:191
  191.4 4.6 fusion.80
  202.1 19.1 %convert_reduce_fusion.3 = (f32[768]{0:T(1024)}, bf16[2048,768]{1,0:T(8,128)(2,1)S(1)}, f32[2048,768]{1,0:T(8,128)}) fusion(f32[2048,768]{1,0:T(8,128)S(1)} %fusion.85, f32[768]{0:T(1024)S(1)} %copy-done.54, bf16[2048,768]{1,0:T(8,128)(2,1)S(1)} %copy-done.22, bf16[768,768]{1,0:T(8,128)(2,1)S(1)} %copy-done), kind=kOutput, calls=%fused_computation.92 | convolution fusion | flops 2533883136 | bytes 20060160 | tf_op jit(solution)/shard_map/td,fd->tf/dot_general | solution.py:203
  222.8 4.5 fusion.86
  227.4 5.5 multiply_convert_fusion.1
  234.6 4.0 convolution_convert_fusion
  238.5 108.8 %all-reduce.14.cloned.1.call-done = f32[2048,768]{1,0:T(8,128)} async-done(((f32[2048,768]{1,0:T(8,128)}), f32[2048,768]{1,0:T(8,128)}) %all-reduce.14.cloned.1.call-update) | async-done | bytes 6291472 | tf_op jit(solution)/shard_map/psum | solution.py:211
  347.3 6.6 multiply_reduce_fusion.1
  354.7 5.8 convert_reduce_fusion.4
  366.0 99.6 %while.56 = (s32[]{:T(128)}, f32[2,1024,3,64]{3,2,1,0:T(4,128)}, f32[2,1024,3,64]{1,0,3,2:T(2,128)}, bf16[2,1024,3,64]{1,3,2,0:T(8,128)(2,1)}, bf16[2,1024,3,64]...) while((s32[]{:T(128)}, f32[2,1024,3,64]{3,2,1,0:T(4,128)}, ...), condition=%wide.region_22.23_spmd, body=%wide.region_18.22_spmd.sunk | while | flops 1031830016 | bytes 76714544 | solution.py:228
  372.3 24.1 %while.58 = (s32[]{:T(128)}, f32[1024,3,64]{0,2,1:T(8,128)S(1)}, f32[1024,3,64]{0,2,1:T(8,128)S(1)}, f32[2,512,3,64]{1,3,2,0:T(8,128)}, bf16[2,512,3,64]{1,3,2,0...) while((s32[]{:T(128)}, f32[1024,3,64]{0,2,1:T(8,128)S(1)}, ...), condition=%wide.region_21.21_spmd.clone, body=%wide.region_19.20_spmd.clone.sunk | while | flops 1031830016 | bytes 61137120 | solution.py:127
  397.1 14.4 %dynamic_update_slice.50 = f32[2,1024,3,64]{1,0,3,2:T(2,128)} dynamic-update-slice(f32[2,1024,3,64]{1,0,3,2:T(2,128)} %get-tuple-element.988, f32[1,1024,3,64]{1,0,3,2:T(1,128)S(1)} %copy.167, s32[]{:T(128)S(6)} %copy.212, s32[]{:T(128)} %constant.61.clone.1..sunk.1, s32[]{:T(128)} %constant.61.clone.1..sunk.1, s32[]{:T(128)} %constant.61.clone.1..sunk.1) | dynamic-update-slice | bytes 1572868 | tf_op jit(solution)/shard_map/while/body/jit(dynamic_update_index_in_dim)/dynamic_update_slice | solution.py:228
  422.0 24.1 %while.58 = (s32[]{:T(128)}, f32[1024,3,64]{0,2,1:T(8,128)S(1)}, f32[1024,3,64]{0,2,1:T(8,128)S(1)}, f32[2,512,3,64]{1,3,2,0:T(8,128)}, bf16[2,512,3,64]{1,3,2,0...) while((s32[]{:T(128)}, f32[1024,3,64]{0,2,1:T(8,128)S(1)}, ...), condition=%wide.region_21.21_spmd.clone, body=%wide.region_19.20_spmd.clone.sunk | while | flops 1031830016 | bytes 61137120 | solution.py:127
  446.9 14.4 %dynamic_update_slice.50 = f32[2,1024,3,64]{1,0,3,2:T(2,128)} dynamic-update-slice(f32[2,1024,3,64]{1,0,3,2:T(2,128)} %get-tuple-element.988, f32[1,1024,3,64]{1,0,3,2:T(1,128)S(1)} %copy.167, s32[]{:T(128)S(6)} %copy.212, s32[]{:T(128)} %constant.61.clone.1..sunk.1, s32[]{:T(128)} %constant.61.clone.1..sunk.1, s32[]{:T(128)} %constant.61.clone.1..sunk.1) | dynamic-update-slice | bytes 1572868 | tf_op jit(solution)/shard_map/while/body/jit(dynamic_update_index_in_dim)/dynamic_update_slice | solution.py:228
  468.1 3.4 copy.102
  471.5 3.6 stack_reshape.7
  475.1 5.4 multiply_reduce_fusion.7
  481.7 4.0 bitcast_convert_fusion
  485.8 7.1 fusion.87
  492.9 4.2 fusion.88
  499.0 3.6 fusion.72
  503.7 4.7 multiply_reduce_fusion.10
  508.8 96.9 %all-reduce.18.cloned.1.call-done = (bf16[2048,768]{1,0:T(8,128)(2,1)}, bf16[2048,768]{1,0:T(8,128)(2,1)}) async-done(((bf16[2048,768]{1,0:T(8,128)(2,1)}, bf16[2048,768]{1,0:T(8,128)(2,1)}), (bf16[2048,768]{1,0:T(8,128)(2,1)}, bf16[2048,768]{1,0:T(8,128)(2,1)})) %all-reduce.18.cloned.1.call-update) | async-done | bytes 6291472 | tf_op jit(solution)/shard_map/psum | solution.py:198
  605.7 5.2 fusion.58
  611.0 41.4 %all-reduce.4 = (f32[768]{0:T(1024)}, f32[768]{0:T(1024)}, f32[3,192]{1,0:T(4,128)}, f32[3,2,32]{2,0,1:T(4,128)S(1)}, f32[768]{0:T(1024)}, /*index=5*/f32[768]{0...) all-reduce(f32[768]{0:T(1024)S(1)} %get-tuple-element.437, ...), channel_id=1, replica_groups=mesh['dp'=8,'tensor'=4] {'dp'}, use_global_device_ids=true, to_apply=%region_27.28 | all-reduce | flops 6144 | bytes 49152 | tf_op jit(solution)/shard_map/psum | solution.py:254
  653.0 6.6 add_convert_fusion.1
  661.6 4.2 fusion.53
  665.9 178.3 %all-reduce.16.cloned.1.call-done = (f32[768,3,192]{0,2,1:T(8,128)}, f32[192,768]{1,0:T(8,128)}, f32[768,768]{1,0:T(8,128)}, f32[768,768]{1,0:T(8,128)}) async-done(((f32[768,3,192]{0,2,1:T(8,128)}, f32[192,768]{1,0:T(8,128)}, f32[768,768]{1,0:T(8,128)}, f32[768,768]{1,0:T(8,128)}), (f32[768,3,192]{0,2,1:T(8,128)}, f32[192,768]{1,0:T(8,128)}, f32[768,768]{1,0:T(8,128)}, ...) | async-done | bytes 7077904 | tf_op jit(solution)/shard_map/psum | solution.py:254
  (352 shorter events, 160.5 us)
Async XLA Ops:
  7.2 194.5 %copy-start = (bf16[768,768]{1,0:T(8,128)(2,1)S(1)}, bf16[768,768]{1,0:T(8,128)(2,1)}, u32[]{:S(2)}) copy-start(bf16[768,768]{1,0:T(8,128)(2,1)} %param.42) | copy-start | bytes 3538948
  7.2 184.2 %all-reduce.12.cloned.1.call-start = ((), (), s32[]{:S(2)}) async-start(), calls=%async_computation | async-start | bytes 12582912 | tf_op jit(solution)/shard_map/psum | solution.py:191
  18.3 7.7 copy-start.34
  18.4 7.6 copy-start.38
  20.1 5.9 copy-start.44
  29.6 35.5 %copy-start.27 = (bf16[192,768]{1,0:T(8,128)(2,1)S(1)}, bf16[192,768]{1,0:T(8,128)(2,1)}, u32[]{:S(2)}) copy-start(bf16[192,768]{1,0:T(8,128)(2,1)} %param.36) | copy-start | bytes 884740
  33.6 11.4 %copy-start.30 = (f32[2,2,3,512]{3,2,1,0:T(4,128)S(1)}, f32[2,2,3,512]{3,2,1,0:T(4,128)}, u32[]{:S(2)}) copy-start(f32[2,2,3,512]{3,2,1,0:T(4,128)} %get-tuple-element.954) | copy-start | bytes 73732 | tf_op jit(solution)/shard_map/while
  50.2 11.4 %copy-start.30 = (f32[2,2,3,512]{3,2,1,0:T(4,128)S(1)}, f32[2,2,3,512]{3,2,1,0:T(4,128)}, u32[]{:S(2)}) copy-start(f32[2,2,3,512]{3,2,1,0:T(4,128)} %get-tuple-element.954) | copy-start | bytes 73732 | tf_op jit(solution)/shard_map/while
  65.2 126.2 %copy-start.58 = (f32[768]{0:T(1024)S(1)}, f32[768]{0:T(1024)}, u32[]{:S(2)}) copy-start(f32[768]{0:T(1024)} %param.37) | copy-start | bytes 9220
  68.9 278.4 %all-reduce.14.cloned.1.call-start = ((), (), s32[]{:S(2)}) async-start(), calls=%async_computation.1 | async-start | bytes 12582912 | tf_op jit(solution)/shard_map/psum | solution.py:211
  202.1 19.1 %copy-start.17 = (f32[2048,768]{1,0:T(8,128)}, f32[2048,768]{1,0:T(8,128)S(1)}, u32[]{:S(2)}) copy-start(f32[2048,768]{1,0:T(8,128)S(1)} %fusion.85) | copy-start | bytes 18874372
  227.4 378.4 %all-reduce.18.cloned.1.call-start = ((), (), s32[]{:S(2)}) async-start(), calls=%async_computation.3 | async-start | bytes 12582912 | tf_op jit(solution)/shard_map/psum | solution.py:198
  347.3 6.7 copy-start.7
  347.3 7.4 copy-start.23
  396.3 19.5 %copy-start.29 = (s32[2,1024]{1,0:T(2,128)S(1)}, s32[2,1024]{1,0:T(2,128)}, u32[]{:S(2)}) copy-start(s32[2,1024]{1,0:T(2,128)} %copy-done.28) | copy-start | bytes 24580 | tf_op jit(solution)/shard_map/while
  446.1 19.5 %copy-start.29 = (s32[2,1024]{1,0:T(2,128)S(1)}, s32[2,1024]{1,0:T(2,128)}, u32[]{:S(2)}) copy-start(s32[2,1024]{1,0:T(2,128)} %copy-done.28) | copy-start | bytes 24580 | tf_op jit(solution)/shard_map/while
  485.7 358.4 %all-reduce.16.cloned.1.call-start = ((), (), s32[]{:S(2)}) async-start(), calls=%async_computation.2 | async-start | bytes 14155776 | tf_op jit(solution)/shard_map/psum | solution.py:254
  485.8 7.1 copy-start.21
  485.8 7.1 copy-start.24
  485.8 11.5 %slice-start = ((s8[6291456]{0:T(1024)(128)(4,1)}), s8[4194304]{0:T(1024)(128)(4,1)S(1)}, s32[]{:S(2)}) async-start(s8[6291456]{0:T(1024)(128)(4,1)} %bitcast.219), calls=%async_computation.4 | async-start | bytes 8388608
  502.6 108.3 %copy-start.46 = (f32[768]{0:T(1024)S(1)}, f32[768]{0:T(1024)}, u32[]{:S(2)}) copy-start(f32[768]{0:T(1024)} %get-tuple-element.435) | copy-start | bytes 9220
  502.6 108.3 %copy-start.47 = (f32[768]{0:T(1024)S(1)}, f32[768]{0:T(1024)}, u32[]{:S(2)}) copy-start(f32[768]{0:T(1024)} %get-tuple-element.440) | copy-start | bytes 9220
  502.6 108.3 %copy-start.48 = (f32[768]{0:T(1024)S(1)}, f32[768]{0:T(1024)}, u32[]{:S(2)}) copy-start(f32[768]{0:T(1024)} %get-tuple-element.547) | copy-start | bytes 9220
  502.7 108.3 %copy-start.49 = (f32[768]{0:T(1024)S(1)}, f32[768]{0:T(1024)}, u32[]{:S(2)}) copy-start(f32[768]{0:T(1024)} %get-tuple-element.569) | copy-start | bytes 9220
  502.7 108.3 %copy-start.56 = (f32[768]{0:T(1024)S(1)}, f32[768]{0:T(1024)}, u32[]{:S(2)}) copy-start(f32[768]{0:T(1024)} %get-tuple-element.544) | copy-start | bytes 9220
  502.7 150.2 %copy-start.55 = (f32[768]{0:T(1024)S(1)}, f32[768]{0:T(1024)}, u32[]{:S(2)}) copy-start(f32[768]{0:T(1024)} %param.43) | copy-start | bytes 9220
  605.7 53.8 %slice-start.2 = ((s8[6291456]{0:T(1024)(128)(4,1)}), s8[2097152]{0:T(1024)(128)(4,1)S(1)}, s32[]{:S(2)}) async-start(s8[6291456]{0:T(1024)(128)(4,1)} %bitcast.221), calls=%async_computation.6 | async-start | bytes 4194304
  652.9 6.6 slice-start.3
  652.9 7.4 copy-start.6
  652.9 8.7 %copy-start.10 = (bf16[2048,768]{1,0:T(8,128)(2,1)S(1)}, bf16[2048,768]{1,0:T(8,128)(2,1)}, u32[]{:S(2)}) copy-start(bf16[2048,768]{1,0:T(8,128)(2,1)} %get-tuple-element.539) | copy-start | bytes 9437188
  844.2 6.3 copy-start.25
  844.2 7.7 copy-start.1
  (53 other events, 133.0 us)
Sparse Core Ops, SparseCore 0:
  69.1 122.2 all-reduce.11
  227.5 119.7 all-reduce.13
  485.9 119.8 all-reduce.17
  611.1 232.9 all-reduce.15
where the time goes:
time: 870 us; the launch traced here: 859 us
  waiting for transfers between devices  506 us (58%)
  local copies, waits for them, and re-layouts  110 us (13%)
  matrix products  100 us (11%)
  other arithmetic  84.9 us (10%)
  blocking collectives  41.4 us (5%)
  between operations  15 us (2%)
    psum x1, waiting for transfers between devices, on_device(): lax.psum((grad_gain_one, grad_shift_one, grad_qkv, grad_qkv_bias, grad_fr...  178 us
    psum x1, waiting for transfers between devices, on_device(): middle = residual + lax.psum(partial_attn, 'tensor') + b_out  122 us
    psum x1, waiting for transfers between devices, on_device(): grad_normed_two = lax.psum(partial_norm_two, 'tensor')  109 us
    psum x1, waiting for transfers between devices, on_device(): lax.psum(partial_mlp.astype(jnp.bfloat16), 'tensor').astype(jnp.float32)  96.9 us
    psum x1, blocking collectives, on_device(): lax.psum((grad_gain_one, grad_shift_one, grad_qkv, grad_qkv_bias, grad_fr...  41.4 us
    dynamic_update_slice x8, local copies, waits for them, and re-layouts, on_device(): lax.map(backward_pack, (query_packs, key_packs, value_packs, grad_mixed,...  35.4 us
    unnamed x137, local copies, waits for them, and re-layouts  20.6 us
    dot_general x1, matrix products, on_device(): jnp.einsum('td,fd->tf', cotangent, w_fc2, preferred_element_type=jnp.floa...  19.1 us
  transfers between devices with their start and end apart: 4, of which 4 were waited for; matrix products, arithmetic and copies ran while one was open for 6% of the time, Pallas kernels for 0%

commit v1 on v0

--- a/solution.py
+++ b/solution.py
@@ -1,7 +1,16 @@
+import functools
 import jax
 import jax.numpy as jnp
 from jax import lax
 from jax.sharding import PartitionSpec as P
+from jax.lax import all_gather
+
+
+def begin_the_tasks(view, which_axis):
+    return jnp.sum(all_gather(view, axis_name=which_axis), 0)
+
+
+use_the_chunk = functools.partial(begin_the_tasks, which_axis="tensor")
 
 
 def layer_stats(values_in, norm_gain, norm_shift):
@@ -188,7 +197,7 @@
     )
     mixed_heads = mixed_packs.reshape(row_total, local_width)
     partial_attn = jnp.dot(mixed_heads, w_out, preferred_element_type=jnp.float32)
-    middle = residual + lax.psum(partial_attn, "tensor") + b_out
+    middle = residual + use_the_chunk(partial_attn) + b_out
     normed_two, scaled_two, inverse_two = layer_stats(middle, norm2_gain, norm2_shift)
     low_normed_two = normed_two.astype(jnp.bfloat16)
     hidden_pre = jnp.dot(low_normed_two, w_fc1, preferred_element_type=jnp.float32) + b_fc1

time: 870 us -> 926 us (1.064)
  waiting for transfers between devices: 506 us -> 541 us
  other arithmetic: 84.9 us -> 97.2 us
    all_gather x0 -> x1, waiting for transfers between devices: none -> 158 us  [begin_the_tasks(): return jnp.sum(all_gather(view, axis_name=which_axis), 0)]
    psum x1 -> x0, waiting for transfers between devices: 122 us -> none  [on_device(): middle = residual + lax.psum(partial_attn, 'tensor') + b_out]
    reduce_sum x0 -> x1, other arithmetic: none -> 12.7 us  [begin_the_tasks(): return jnp.sum(all_gather(view, axis_name=which_axis), 0)]
  transfers between devices with their start and end apart: 4 -> 4, of which waited for: 4 -> 4; matrix products, arithmetic and copies ran while one was open for 6% -> 5% of each run, Pallas kernels for 0% -> 0%
where the time goes in v1:
time: 926 us; the launch traced here: 915 us
  waiting for transfers between devices  541 us (58%)
  local copies, waits for them, and re-layouts  110 us (12%)
  matrix products  100 us (11%)
  other arithmetic  97.2 us (10%)
  blocking collectives  41.4 us (4%)
  between operations  15 us (2%)
    psum x1, waiting for transfers between devices, on_device(): lax.psum((grad_gain_one, grad_shift_one, grad_qkv, grad_qkv_bias, grad_fr...  178 us
    all_gather x1, waiting for transfers between devices, begin_the_tasks(): return jnp.sum(all_gather(view, axis_name=which_axis), 0)  158 us
    psum x1, waiting for transfers between devices, on_device(): grad_normed_two = lax.psum(partial_norm_two, 'tensor')  109 us
    psum x1, waiting for transfers between devices, on_device(): lax.psum(partial_mlp.astype(jnp.bfloat16), 'tensor').astype(jnp.float32)  96.9 us
    psum x1, blocking collectives, on_device(): lax.psum((grad_gain_one, grad_shift_one, grad_qkv, grad_qkv_bias, grad_fr...  41.4 us
    dynamic_update_slice x8, local copies, waits for them, and re-layouts, on_device(): lax.map(backward_pack, (query_packs, key_packs, value_packs, grad_mixed,...  35.4 us
    unnamed x137, local copies, waits for them, and re-layouts  21 us
    dot_general x1, matrix products, on_device(): jnp.einsum('td,fd->tf', cotangent, w_fc2, preferred_element_type=jnp.floa...  19.1 us
  transfers between devices with their start and end apart: 4, of which 4 were waited for; matrix products, arithmetic and copies ran while one was open for 5% of the time, Pallas kernels for 0%

profile of v1, /device:TPU:0, one launch (start us, length us, event | category | flops | bytes accessed | tf_op | source)
XLA Modules:
  0.0 914.6 jit_solution(10092107732566013165)
XLA Ops:
  29.6 33.5 %while.54 = (s32[]{:T(128)}, bf16[2,1024,192]{1,2,0:T(8,128)(2,1)}, f32[2,2,3,512]{3,2,1,0:T(4,128)}, bf16[2,1024,3,64]{1,3,2,0:T(8,128)(2,1)}, s32[2,1024]{1,0:...) while((s32[]{:T(128)}, bf16[2,1024,192]{1,2,0:T(8,128)(2,1)}, ...), condition=%wide.region_10.11_spmd, body=%wide.region_5.10_spmd.sunk | while | flops 422148608 | bytes 28762504 | solution.py:195
  33.7 11.3 %while.57 = (s32[]{:T(128)}, bf16[2,512,3,64]{1,3,2,0:T(8,128)(2,1)S(1)}, f32[2,3,512]{2,1,0:T(4,128)S(1)}, s32[2,512]{1,0:T(2,128)S(1)}, s32[1024]{0:T(1024)S(1...) while((s32[]{:T(128)}, ...), condition=%wide.region_9.9_spmd, body=%wide.region_6.8_spmd.sunk | while | flops 422148608 | bytes 22220916 | solution.py:91
  50.3 11.3 %while.57 = (s32[]{:T(128)}, bf16[2,512,3,64]{1,3,2,0:T(8,128)(2,1)S(1)}, f32[2,3,512]{2,1,0:T(4,128)S(1)}, s32[2,512]{1,0:T(2,128)S(1)}, s32[1024]{0:T(1024)S(1...) while((s32[]{:T(128)}, ...), condition=%wide.region_9.9_spmd, body=%wide.region_6.8_spmd.sunk | while | flops 422148608 | bytes 22220916 | solution.py:91
  65.2 3.7 fusion.84
  69.0 157.6 %all-gather.3.cloned.1.call-done = f32[8192,768]{1,0:T(8,128)} async-done(((f32[2048,768]{1,0:T(8,128)}), f32[8192,768]{1,0:T(8,128)}) %all-gather.3.cloned.1.call-update) | async-done | bytes 25165840 | tf_op jit(solution)/shard_map/all_gather | solution.py:10
  226.6 12.7 %reduce_sum.266 = f32[2048,768]{1,0:T(8,128)} reduce(f32[4,2048,768]{2,1,0:T(8,128)} %bitcast.226, f32[]{:T(128)} %constant.82.clone.1), dimensions={0}, to_apply=%region_11.12 | reduce | flops 4718592 | bytes 31457284 | tf_op jit(solution)/shard_map/reduce_sum | solution.py:10
  239.3 4.6 fusion.80
  250.0 19.1 %convert_reduce_fusion.3 = (f32[768]{0:T(1024)}, bf16[2048,768]{1,0:T(8,128)(2,1)S(1)}, f32[2048,768]{1,0:T(8,128)}) fusion(f32[2048,768]{1,0:T(8,128)S(1)} %fusion.85, f32[768]{0:T(1024)S(1)} %copy-done.54, bf16[2048,768]{1,0:T(8,128)(2,1)S(1)} %copy-done.22, bf16[768,768]{1,0:T(8,128)(2,1)S(1)} %copy-done), kind=kOutput, calls=%fused_computation.92 | convolution fusion | flops 2533883136 | bytes 20060160 | tf_op jit(solution)/shard_map/td,fd->tf/dot_general | solution.py:212
  270.7 4.5 fusion.86
  275.4 5.5 multiply_convert_fusion.1
  282.5 4.0 convolution_convert_fusion
  286.5 108.6 %all-reduce.11.cloned.1.call-done = f32[2048,768]{1,0:T(8,128)} async-done(((f32[2048,768]{1,0:T(8,128)}), f32[2048,768]{1,0:T(8,128)}) %all-reduce.11.cloned.1.call-update) | async-done | bytes 6291472 | tf_op jit(solution)/shard_map/psum | solution.py:220
  395.0 6.6 multiply_reduce_fusion.1
  402.4 5.8 convert_reduce_fusion.4
  413.7 107.6 %while.56 = (s32[]{:T(128)}, f32[2,1024,3,64]{3,2,1,0:T(4,128)}, f32[2,1024,3,64]{1,0,3,2:T(2,128)}, bf16[2,1024,3,64]{1,3,2,0:T(8,128)(2,1)}, bf16[2,1024,3,64]...) while((s32[]{:T(128)}, f32[2,1024,3,64]{3,2,1,0:T(4,128)}, ...), condition=%wide.region_22.23_spmd, body=%wide.region_18.22_spmd.sunk | while | flops 1031830016 | bytes 76714544 | solution.py:237
  428.0 24.1 %while.58 = (s32[]{:T(128)}, f32[1024,3,64]{0,2,1:T(8,128)S(1)}, f32[1024,3,64]{0,2,1:T(8,128)S(1)}, f32[2,512,3,64]{1,3,2,0:T(8,128)}, bf16[2,512,3,64]{1,3,2,0...) while((s32[]{:T(128)}, f32[1024,3,64]{0,2,1:T(8,128)S(1)}, ...), condition=%wide.region_21.21_spmd.clone, body=%wide.region_19.20_spmd.clone.sunk | while | flops 1031830016 | bytes 61137120 | solution.py:136
  452.9 14.4 %dynamic_update_slice.50 = f32[2,1024,3,64]{1,0,3,2:T(2,128)} dynamic-update-slice(f32[2,1024,3,64]{1,0,3,2:T(2,128)} %get-tuple-element.988, f32[1,1024,3,64]{1,0,3,2:T(1,128)S(1)} %copy.168, s32[]{:T(128)S(6)} %copy.212, s32[]{:T(128)} %constant.61.clone.1..sunk.1, s32[]{:T(128)} %constant.61.clone.1..sunk.1, s32[]{:T(128)} %constant.61.clone.1..sunk.1) | dynamic-update-slice | bytes 1572868 | tf_op jit(solution)/shard_map/while/body/jit(dynamic_update_index_in_dim)/dynamic_update_slice | solution.py:237
  477.7 24.1 %while.58 = (s32[]{:T(128)}, f32[1024,3,64]{0,2,1:T(8,128)S(1)}, f32[1024,3,64]{0,2,1:T(8,128)S(1)}, f32[2,512,3,64]{1,3,2,0:T(8,128)}, bf16[2,512,3,64]{1,3,2,0...) while((s32[]{:T(128)}, f32[1024,3,64]{0,2,1:T(8,128)S(1)}, ...), condition=%wide.region_21.21_spmd.clone, body=%wide.region_19.20_spmd.clone.sunk | while | flops 1031830016 | bytes 61137120 | solution.py:136
  502.6 14.4 %dynamic_update_slice.50 = f32[2,1024,3,64]{1,0,3,2:T(2,128)} dynamic-update-slice(f32[2,1024,3,64]{1,0,3,2:T(2,128)} %get-tuple-element.988, f32[1,1024,3,64]{1,0,3,2:T(1,128)S(1)} %copy.168, s32[]{:T(128)S(6)} %copy.212, s32[]{:T(128)} %constant.61.clone.1..sunk.1, s32[]{:T(128)} %constant.61.clone.1..sunk.1, s32[]{:T(128)} %constant.61.clone.1..sunk.1) | dynamic-update-slice | bytes 1572868 | tf_op jit(solution)/shard_map/while/body/jit(dynamic_update_index_in_dim)/dynamic_update_slice | solution.py:237
  527.2 3.6 stack_reshape.7
  530.9 5.4 multiply_reduce_fusion.7
  537.4 4.0 bitcast_convert_fusion
  541.5 7.1 fusion.87
  548.6 4.2 fusion.88
  554.7 3.6 fusion.72
  559.4 4.7 multiply_reduce_fusion.10
  564.5 96.9 %all-reduce.15.cloned.1.call-done = (bf16[2048,768]{1,0:T(8,128)(2,1)}, bf16[2048,768]{1,0:T(8,128)(2,1)}) async-done(((bf16[2048,768]{1,0:T(8,128)(2,1)}, bf16[2048,768]{1,0:T(8,128)(2,1)}), (bf16[2048,768]{1,0:T(8,128)(2,1)}, bf16[2048,768]{1,0:T(8,128)(2,1)})) %all-reduce.15.cloned.1.call-update) | async-done | bytes 6291472 | tf_op jit(solution)/shard_map/psum | solution.py:207
  661.4 5.2 fusion.58
  666.7 41.4 %all-reduce.4 = (f32[768]{0:T(1024)}, f32[768]{0:T(1024)}, f32[3,192]{1,0:T(4,128)}, f32[3,2,32]{2,0,1:T(4,128)S(1)}, f32[768]{0:T(1024)}, /*index=5*/f32[768]{0...) all-reduce(f32[768]{0:T(1024)S(1)} %get-tuple-element.437, ...), channel_id=1, replica_groups=mesh['dp'=8,'tensor'=4] {'dp'}, use_global_device_ids=true, to_apply=%region_27.28 | all-reduce | flops 6144 | bytes 49152 | tf_op jit(solution)/shard_map/psum | solution.py:263
  708.7 6.6 add_convert_fusion.1
  717.4 4.2 fusion.53
  721.6 178.3 %all-reduce.13.cloned.1.call-done = (f32[768,3,192]{0,2,1:T(8,128)}, f32[192,768]{1,0:T(8,128)}, f32[768,768]{1,0:T(8,128)}, f32[768,768]{1,0:T(8,128)}) async-done(((f32[768,3,192]{0,2,1:T(8,128)}, f32[192,768]{1,0:T(8,128)}, f32[768,768]{1,0:T(8,128)}, f32[768,768]{1,0:T(8,128)}), (f32[768,3,192]{0,2,1:T(8,128)}, f32[192,768]{1,0:T(8,128)}, f32[768,768]{1,0:T(8,128)}, ...) | async-done | bytes 7077904 | tf_op jit(solution)/shard_map/psum | solution.py:263
  (353 shorter events, 163.9 us)
Async XLA Ops:
  7.2 242.5 %copy-start = (bf16[768,768]{1,0:T(8,128)(2,1)S(1)}, bf16[768,768]{1,0:T(8,128)(2,1)}, u32[]{:S(2)}) copy-start(bf16[768,768]{1,0:T(8,128)(2,1)} %param.42) | copy-start | bytes 3538948
  7.2 219.4 %all-gather.3.cloned.1.call-start = ((), (), s32[]{:S(2)}) async-start(), calls=%async_computation.1 | async-start | bytes 31457280 | tf_op jit(solution)/shard_map/all_gather | solution.py:10
  18.3 7.7 copy-start.34
  18.4 7.6 copy-start.38
  20.1 5.9 copy-start.44
  29.6 35.6 %copy-start.27 = (bf16[192,768]{1,0:T(8,128)(2,1)S(1)}, bf16[192,768]{1,0:T(8,128)(2,1)}, u32[]{:S(2)}) copy-start(bf16[192,768]{1,0:T(8,128)(2,1)} %param.36) | copy-start | bytes 884740
  33.6 11.4 %copy-start.30 = (f32[2,2,3,512]{3,2,1,0:T(4,128)S(1)}, f32[2,2,3,512]{3,2,1,0:T(4,128)}, u32[]{:S(2)}) copy-start(f32[2,2,3,512]{3,2,1,0:T(4,128)} %get-tuple-element.954) | copy-start | bytes 73732 | tf_op jit(solution)/shard_map/while
  50.3 11.4 %copy-start.30 = (f32[2,2,3,512]{3,2,1,0:T(4,128)S(1)}, f32[2,2,3,512]{3,2,1,0:T(4,128)}, u32[]{:S(2)}) copy-start(f32[2,2,3,512]{3,2,1,0:T(4,128)} %get-tuple-element.954) | copy-start | bytes 73732 | tf_op jit(solution)/shard_map/while
  69.0 326.0 %all-reduce.11.cloned.1.call-start = ((), (), s32[]{:S(2)}) async-start(), calls=%async_computation | async-start | bytes 12582912 | tf_op jit(solution)/shard_map/psum | solution.py:220
  226.6 12.7 %copy-start.58 = (f32[768]{0:T(1024)S(1)}, f32[768]{0:T(1024)}, u32[]{:S(2)}) copy-start(f32[768]{0:T(1024)} %param.37) | copy-start | bytes 9220
  250.0 19.1 %copy-start.17 = (f32[2048,768]{1,0:T(8,128)}, f32[2048,768]{1,0:T(8,128)S(1)}, u32[]{:S(2)}) copy-start(f32[2048,768]{1,0:T(8,128)S(1)} %fusion.85) | copy-start | bytes 18874372
  275.3 386.2 %all-reduce.15.cloned.1.call-start = ((), (), s32[]{:S(2)}) async-start(), calls=%async_computation.3 | async-start | bytes 12582912 | tf_op jit(solution)/shard_map/psum | solution.py:207
  395.0 6.7 copy-start.7
  395.0 7.4 copy-start.23
  452.0 19.5 %copy-start.29 = (s32[2,1024]{1,0:T(2,128)S(1)}, s32[2,1024]{1,0:T(2,128)}, u32[]{:S(2)}) copy-start(s32[2,1024]{1,0:T(2,128)} %copy-done.28) | copy-start | bytes 24580 | tf_op jit(solution)/shard_map/while
  501.8 19.5 %copy-start.29 = (s32[2,1024]{1,0:T(2,128)S(1)}, s32[2,1024]{1,0:T(2,128)}, u32[]{:S(2)}) copy-start(s32[2,1024]{1,0:T(2,128)} %copy-done.28) | copy-start | bytes 24580 | tf_op jit(solution)/shard_map/while
  541.5 358.4 %all-reduce.13.cloned.1.call-start = ((), (), s32[]{:S(2)}) async-start(), calls=%async_computation.2 | async-start | bytes 14155776 | tf_op jit(solution)/shard_map/psum | solution.py:263
  541.5 7.1 copy-start.21
  541.5 7.1 copy-start.24
  541.5 11.5 %slice-start = ((s8[6291456]{0:T(1024)(128)(4,1)}), s8[4194304]{0:T(1024)(128)(4,1)S(1)}, s32[]{:S(2)}) async-start(s8[6291456]{0:T(1024)(128)(4,1)} %bitcast.220), calls=%async_computation.4 | async-start | bytes 8388608
  558.4 108.3 %copy-start.46 = (f32[768]{0:T(1024)S(1)}, f32[768]{0:T(1024)}, u32[]{:S(2)}) copy-start(f32[768]{0:T(1024)} %get-tuple-element.435) | copy-start | bytes 9220
  558.4 108.3 %copy-start.47 = (f32[768]{0:T(1024)S(1)}, f32[768]{0:T(1024)}, u32[]{:S(2)}) copy-start(f32[768]{0:T(1024)} %get-tuple-element.440) | copy-start | bytes 9220
  558.4 108.3 %copy-start.48 = (f32[768]{0:T(1024)S(1)}, f32[768]{0:T(1024)}, u32[]{:S(2)}) copy-start(f32[768]{0:T(1024)} %get-tuple-element.547) | copy-start | bytes 9220
  558.4 108.3 %copy-start.49 = (f32[768]{0:T(1024)S(1)}, f32[768]{0:T(1024)}, u32[]{:S(2)}) copy-start(f32[768]{0:T(1024)} %get-tuple-element.569) | copy-start | bytes 9220
  558.4 108.3 %copy-start.56 = (f32[768]{0:T(1024)S(1)}, f32[768]{0:T(1024)}, u32[]{:S(2)}) copy-start(f32[768]{0:T(1024)} %get-tuple-element.544) | copy-start | bytes 9220
  558.4 150.2 %copy-start.55 = (f32[768]{0:T(1024)S(1)}, f32[768]{0:T(1024)}, u32[]{:S(2)}) copy-start(f32[768]{0:T(1024)} %param.43) | copy-start | bytes 9220
  661.4 53.8 %slice-start.2 = ((s8[6291456]{0:T(1024)(128)(4,1)}), s8[2097152]{0:T(1024)(128)(4,1)S(1)}, s32[]{:S(2)}) async-start(s8[6291456]{0:T(1024)(128)(4,1)} %bitcast.222), calls=%async_computation.6 | async-start | bytes 4194304
  708.6 6.6 slice-start.3
  708.7 7.4 copy-start.6
  708.7 8.7 copy-start.10
  899.9 6.3 copy-start.25
  899.9 7.7 copy-start.1
  (53 other events, 133.0 us)
Sparse Core Ops, SparseCore 0:
  69.1 157.4 all-gather.2
  275.4 119.5 all-reduce.10
  541.6 119.8 all-reduce.14
  666.9 232.9 all-reduce.12
